TPU v7x, 32 devices: a whole 2x2x4 slice. The times are simulated.
32 devices in a mesh: cfg: 2 (over y), space: 4 (over z), tm: 4 (over x, core).
Axes of the slice: x: 2, y: 2, z: 4, core: 2. Of those that a mesh axis runs over, the one named last changes fastest.
Arguments:
- solutions: bfloat16 [16, 128, 32, 3072], P(('cfg', 'tm'), None, None, 'space'), parts along dimension 0, may hold values from -6 to 6
- eigvecs: bfloat16 [16, 2, 128, 3072], P(('cfg', 'tm'), None, 'space'), parts along dimension 0, may hold values from -0.078125 to 0.078125
- source_time: int32 [256], P('cfg'), parts along dimension 0, may hold values from 0 to 7
Outputs:
- perambulator: bfloat16 [16, 128, 32, 128], P(('cfg', 'tm'), 'space'), parts along dimension 0
There are 2 independent parts, one for each index of `cfg`. A program takes and returns all parts, laid end to end along the dimension named above; each array names one. Nothing has to cross between parts.
All inputs are finite; a program needn't handle non-finite values.
Results may differ from a plain program's by a relative error of at most 0.001.
Values may be sent and summed in bfloat16 or wider, within the bound.
A program may use at most 128 MiB of HBM per device.

v0:
```python
import jax
import jax.numpy as jnp
from jax import lax
from jax.sharding import PartitionSpec as P


def contract_block(spinors, vectors):
    slices = spinors.shape[0]
    sources = spinors.shape[1]
    count = vectors.shape[2]
    stacked = vectors.reshape(slices, 2 * count, vectors.shape[3])
    products = jnp.einsum(
        "tkc,tjc->tkj",
        spinors.reshape(slices, sources * 32, spinors.shape[3]),
        stacked,
        preferred_element_type=jnp.float32,
    )
    products = products.reshape(slices, sources, 2, 16, 2, count)
    real_part = products[:, :, 0, :, 0, :] + products[:, :, 1, :, 1, :]
    imag_part = products[:, :, 1, :, 0, :] - products[:, :, 0, :, 1, :]
    return jnp.concatenate([real_part, imag_part], axis=2)


def shards(solutions, eigvecs, source_time):
    slices = solutions.shape[0]
    local_vectors = lax.all_to_all(eigvecs, "space", split_axis=3, concat_axis=2, tiled=True)
    partial_value = contract_block(solutions, local_vectors)
    sums = lax.psum_scatter(partial_value, "space", scatter_dimension=1, tiled=True)
    owned = sums.shape[1]
    first_source = lax.axis_index("space") * owned
    owned_times = lax.dynamic_slice_in_dim(source_time, first_source, owned)
    slice_index = lax.axis_index("tm") * slices + jnp.arange(slices, dtype=jnp.int32)
    signs = jnp.where(slice_index[:, None] < owned_times[None, :], -1.0, 1.0).astype(jnp.float32)
    return (sums * signs[:, :, None, None]).astype(jnp.bfloat16)


def solution(mesh):
    return jax.shard_map(
        shards,
        mesh=mesh,
        in_specs=(
            P(("cfg", "tm"), None, None, "space"),
            P(("cfg", "tm"), None, "space", None),
            P("cfg"),
        ),
        out_specs=P(("cfg", "tm"), "space", None, None),
        check_vma=False,
    )
```

profile of v0, /device:TPU:0, one launch (start us, length us, event | category | flops | bytes accessed | tf_op | source)
XLA Modules:
  0.0 179.1 jit_solution(6981386661717572682)
XLA Ops:
  6.5 0.0 reduce-scatter.5.cloned.1.call-start
  6.5 7.5 %copy.9 = bf16[2,2,32,3072]{2,1,0,3:T(2,128)(2,1)S(1)} copy(bf16[2,2,32,3072]{3,2,1,0:T(8,128)(2,1)} %param.4) | data formatting | bytes 1572864 | tf_op args[1]
  14.0 3.8 %reshape.48 = bf16[4,2,49152]{2,1,0:T(2,128)(2,1)} reshape(bf16[3072,2,2,32]{3,2,1,0:T(2,128)(2,1)S(1)} %bitcast.34) | data formatting | bytes 1572864
  17.8 26.6 %all_to_all.15 = bf16[4,2,49152]{2,1,0:T(2,128)(2,1)} all-to-all(bf16[4,2,49152]{2,1,0:T(2,128)(2,1)} %reshape.48), channel_id=1, replica_groups=mesh['cfg'=2,'space'=4,'tm'=4] {'space'}, dimensions={0} | all-to-all | bytes 1572864 | tf_op jit(solution)/shard_map/all_to_all | solution.py:26
  44.4 3.2 %reshape.49 = bf16[3072,2,2,32]{3,2,1,0:T(2,128)(2,1)S(1)} reshape(bf16[4,2,49152]{2,1,0:T(2,128)(2,1)} %all_to_all.15) | data formatting | bytes 1572864
  47.6 6.1 %copy.10 = bf16[2,2,32,4,768]{4,2,3,1,0:T(8,128)(2,1)} copy(bf16[2,2,32,4,768]{2,1,0,4,3:T(2,128)(2,1)S(1)} %bitcast.33) | data formatting | bytes 1572864 | tf_op jit(solution)/shard_map/all_to_all | solution.py:26
  53.7 11.4 %fusion.2 = f32[2,4096,256]{2,1,0:T(8,128)} fusion(bf16[2,4096,768]{2,1,0:T(8,128)(2,1)} %bitcast.32, bf16[2,256,768]{2,1,0:T(8,128)(2,1)} %bitcast.40), kind=kOutput, calls=%fused_computation.9 | convolution fusion | flops 3221225472 | bytes 21757952 | tf_op jit(solution)/shard_map/tkc,tjc->tkj/dot_general | solution.py:12
  65.1 10.8 %reshape.45 = f32[2,128,2,16,2,128]{5,4,3,2,1,0:T(2,128)} reshape(f32[2,4096,256]{2,1,0:T(8,128)} %fusion.2) | data formatting | bytes 16777216 | tf_op jit(solution)/shard_map/reshape | solution.py:18
  75.8 11.1 %fusion.1 = (f32[2,128,1,16,1,128]{5,4,3,2,1,0:T(1,128)S(1)}, f32[2,128,1,16,1,128]{5,4,3,2,1,0:T(1,128)S(1)}, f32[2,128,1,16,1,128]{5,4,3,2,1,0:T(1,128)S(1)}, f32[2,128,1,16,1,128]{5,4,3,2,1,0:T(1,128)S(1)}) fusion(f32[2,128,2,16,2,128]{5,4,3,2,1,0:T(2,128)} %reshape.45), kind=kLoop, calls=%fused_computation.8 | loop fusion | bytes 16777216 | tf_op jit(solution)/shard_map/slice | solution.py:19
  87.0 0.5 subtract_bitcast_fusion
  87.5 0.5 pad_maximum_fusion
  88.0 0.5 copy.15
  88.5 5.2 %copy.27 = f32[16,8,64,128]{3,1,2,0:T(8,128)} copy(f32[16,8,64,128]{3,2,1,0:T(8,128)S(1)} %bitcast.31) | data formatting | bytes 8388608
  93.8 0.0 copy-start
  93.8 0.0 reduce-scatter.5.cloned.1.call-update
  93.8 0.6 copy-done
  94.4 0.1 dynamic_slice.3
  94.5 0.1 compare_select_fusion
  94.6 75.3 %reduce-scatter.5.cloned.1.call-done = f32[32,8192]{1,0:T(8,128)} async-done(((f32[128,8192]{1,0:T(8,128)}), f32[32,8192]{1,0:T(8,128)}) %reduce-scatter.5.cloned.1.call-update) | async-done | bytes 1048592
  169.8 1.4 copy.22
  171.3 0.9 fusion
  (1 shorter events, 0.0 us)
Async XLA Ops:
  6.5 163.3 %reduce-scatter.5.cloned.1.call-start = ((), (), s32[]{:S(2)}) async-start(), calls=%async_computation.2 | async-start | bytes 5242880
  93.8 0.7 copy-start
Sparse Core Ops, SparseCore 0:
  93.9 75.8 reduce-scatter.4
where the time goes:
time: 180 us; the launch traced here: 179 us
  waiting for transfers between devices  75.3 us (42%)
  local copies, waits for them, and re-layouts  50.3 us (28%)
  blocking collectives  26.6 us (15%)
  between operations  13.5 us (8%)
  matrix products  11.4 us (6%)
  other arithmetic  2.09 us (1%)
    unnamed x2, waiting for transfers between devices  75.3 us
    all_to_all x1, blocking collectives, shards(): lax.all_to_all(eigvecs, 'space', split_axis=3, concat_axis=2, tiled=True)  26.6 us
    unnamed x8, local copies, waits for them, and re-layouts  22.2 us
    dot_general x1, matrix products, contract_block(): jnp.einsum('tkc,tjc->tkj', spinors.reshape(slices, sources * 32, spinors....  11.4 us
    slice x1, local copies, waits for them, and re-layouts, contract_block(): real_part = products[:, :, 0, :, 0, :] + products[:, :, 1, :, 1, :]  11.1 us
    reshape x1, local copies, waits for them, and re-layouts, contract_block(): products = products.reshape(slices, sources, 2, 16, 2, count)  10.8 us
    all_to_all x1, local copies, waits for them, and re-layouts, shards(): lax.all_to_all(eigvecs, 'space', split_axis=3, concat_axis=2, tiled=True)  6.11 us
  transfers between devices with their start and end apart: 1, of which 1 were waited for; matrix products, arithmetic and copies ran while one was open for 0% of the time, Pallas kernels for 0%

commit v1 on v0

v1 whole, which is shorter than its diff:
```python
import functools

import jax
import jax.numpy as jnp
from jax import lax
from jax.experimental import pallas as pl
from jax.experimental.pallas import tpu as pltpu
from jax.sharding import PartitionSpec as P

MESH = pl.DeviceIdType.MESH
LEVELS = 32767.0


def kernel(n, time_ref, sol_ref, eig_ref, out_ref, sol_v, eig_v, w_v, part, own, code, scale, code_in, scale_in,
           sol_sem, own_sem, eig_send, eig_recv, code_send, scale_send, code_recv, scale_recv):
    me = lax.axis_index("space")
    slices, sources, spins, cols = sol_v.shape
    count = eig_ref.shape[2]
    vectors = n * count
    owned = sources // n
    half = spins // 2

    barrier = pltpu.get_barrier_semaphore()
    for o in range(1, n):
        pl.semaphore_signal(barrier, inc=1, device_id={"space": lax.rem(me + o, n)}, device_id_type=MESH)

    def block_of(d):
        return pl.ds(pl.multiple_of(d * cols, cols), cols)

    def eig_own(t):
        return pltpu.make_async_copy(eig_ref.at[t, :, :, block_of(me)], eig_v.at[t, me], own_sem.at[t])

    def sol_copy(t, d):
        rows = pl.ds(d * owned, owned)
        return pltpu.make_async_copy(sol_ref.at[t, rows], sol_v.at[t, rows], sol_sem.at[t, d])

    def eig_copy(t, o, dst):
        to = lax.rem(me + o, n)
        return pltpu.make_async_remote_copy(
            eig_ref.at[t, :, :, block_of(to)], eig_v.at[t, dst], eig_send.at[t, o], eig_recv.at[t, o],
            device_id={"space": to}, device_id_type=MESH)

    for t in range(slices):
        eig_own(t).start()

    def start_sol(t):
        def body(d, _):
            sol_copy(t, d).start()
            return 0
        lax.fori_loop(0, n, body, 0)

    start_sol(0)
    pl.semaphore_wait(barrier, n - 1)
    for o in range(1, n):
        eig_copy(0, o, me).start()
    for t in range(1, slices):
        start_sol(t)

    def partial_sum(t, d, dst):
        block = sol_v[t, pl.ds(d * owned, owned)].reshape(owned * spins, cols)
        p = lax.dot_general(block, w_v[t], (((1,), (1,)), ((), ())), preferred_element_type=jnp.float32)
        p = p.reshape(owned, 2, half, 2 * vectors)
        dst[:, :half, :] = p[:, 0, :, :vectors] + p[:, 1, :, vectors:]
        dst[:, half:, :] = p[:, 1, :, :vectors] - p[:, 0, :, vectors:]

    def chunk_copies(way, t, d):
        to = lax.rem(jnp.where(way == 0, me + 1, me + n - 1), n)
        return [
            pltpu.make_async_remote_copy(src.at[t, d], dst.at[way, t, d], s.at[t, d], r.at[way, t, d],
                                         device_id={"space": to}, device_id_type=MESH)
            for src, dst, s, r in ((code, code_in, code_send, code_recv), (scale, scale_in, scale_send, scale_recv))
        ]

    def received(way, t, d):
        for c in chunk_copies(way, t, d):
            c.wait_recv()
        return code_in[way, t, d].astype(jnp.int32).astype(jnp.float32) * scale_in[way, t, d][:1][None]

    def emit(t):
        def body(j, _):
            k = j // 2
            way = jnp.where(me < n // 2, j % 2, 1 - j % 2)
            d = jnp.where(way == 0, n - 1 - k, k)

            @pl.when(jnp.where(way == 0, d - me, me - d) > 0)
            def _():
                partial_sum(t, d, part)

                @pl.when(jnp.where(way == 0, me, n - 1 - me) > 0)
                def _():
                    part[...] += received(way, t, d)

                x = part[...]
                top = jnp.maximum(jnp.max(jnp.max(jnp.abs(x), axis=0), axis=0, keepdims=True), 1e-33)
                code[t, d] = jnp.round(x * (LEVELS / top)[None]).astype(jnp.int32).astype(jnp.int16)
                scale[t, d] = jnp.broadcast_to(top * (1.0 / LEVELS), (8, vectors))
                for c in chunk_copies(way, t, d):
                    c.start()
            return 0

        lax.fori_loop(0, 2 * (n - 1), body, 0)

    for t in range(slices):
        for o in range(1, n):
            eig_copy(t, o, me).wait_send()
        if t + 1 < slices:
            for o in range(1, n):
                eig_copy(t + 1, o, me).start()
        for o in range(1, n):
            eig_copy(t, o, lax.rem(me + n - o, n)).wait_recv()
        eig_own(t).wait()
        for c in range(2):
            w_v[t, c * vectors:(c + 1) * vectors, :] = (
                eig_v[t, :, c].astype(jnp.float32).reshape(vectors, cols).astype(jnp.bfloat16))

        def wait_sol(d, _):
            sol_copy(t, d).wait()
            return 0

        lax.fori_loop(0, n, wait_sol, 0)
        emit(t)
        partial_sum(t, me, own.at[t])

    for t in range(slices):
        @pl.when(me > 0)
        def _():
            own[t] += received(0, t, me)

        @pl.when(me < n - 1)
        def _():
            own[t] += received(1, t, me)

        now = lax.axis_index("tm") * slices + t

        def finish(i, _):
            sign = jnp.where(now < time_ref[me * owned + i], -1.0, 1.0)
            out_ref[t, i] = (own[t, i] * sign).astype(jnp.bfloat16)
            return 0

        lax.fori_loop(0, owned, finish, 0)

    def drain(j, _):
        t, d = j // n, j % n

        @pl.when(d != me)
        def _():
            for c in chunk_copies(jnp.where(d > me, 0, 1), t, d):
                c.wait_send()
        return 0

    lax.fori_loop(0, slices * n, drain, 0)


def shards(n, solutions, eigvecs, source_time):
    slices, sources, spins, cols = solutions.shape
    count = eigvecs.shape[2]
    vectors = n * count
    owned = sources // n
    dma = pltpu.SemaphoreType.DMA
    return pl.pallas_call(
        functools.partial(kernel, n),
        out_shape=jax.ShapeDtypeStruct((slices, owned, spins, vectors), jnp.bfloat16),
        in_specs=[
            pl.BlockSpec(memory_space=pltpu.SMEM),
            pl.BlockSpec(memory_space=pl.ANY),
            pl.BlockSpec(memory_space=pl.ANY),
        ],
        out_specs=pl.BlockSpec(memory_space=pltpu.VMEM),
        scratch_shapes=[
            pltpu.VMEM((slices, sources, spins, cols), jnp.bfloat16),
            pltpu.VMEM((slices, n, 2, count, cols), jnp.bfloat16),
            pltpu.VMEM((slices, 2 * vectors, cols), jnp.bfloat16),
            pltpu.VMEM((owned, spins, vectors), jnp.float32),
            pltpu.VMEM((slices, owned, spins, vectors), jnp.float32),
            pltpu.VMEM((slices, n, owned, spins, vectors), jnp.int16),
            pltpu.VMEM((slices, n, 8, vectors), jnp.float32),
            pltpu.VMEM((2, slices, n, owned, spins, vectors), jnp.int16),
            pltpu.VMEM((2, slices, n, 8, vectors), jnp.float32),
            dma((slices, n)),
            dma((slices,)),
            dma((slices, n)),
            dma((slices, n)),
            dma((slices, n)),
            dma((slices, n)),
            dma((2, slices, n)),
            dma((2, slices, n)),
        ],
        compiler_params=pltpu.CompilerParams(
            collective_id=0, has_side_effects=True, vmem_limit_bytes=48 << 20),
    )(source_time, solutions, eigvecs)


def solution(mesh):
    return jax.shard_map(
        functools.partial(shards, mesh.shape["space"]),
        mesh=mesh,
        in_specs=(
            P(("cfg", "tm"), None, None, "space"),
            P(("cfg", "tm"), None, "space", None),
            P("cfg"),
        ),
        out_specs=P(("cfg", "tm"), "space", None, None),
        check_vma=False,
    )
```

time: 180 us -> 62.9 us (0.35)
  waiting for transfers between devices: 75.3 us -> 0 us
  Pallas kernels: 0 us -> 60.1 us
  local copies, waits for them, and re-layouts: 50.3 us -> 2.58 us
  blocking collectives: 26.6 us -> 0 us
  between operations: 13.5 us -> 0.01 us
  matrix products: 11.4 us -> 0 us
  other arithmetic: 2.09 us -> 0 us
    unnamed x2 -> x0, waiting for transfers between devices: 75.3 us -> none
    pallas_call x0 -> x1, Pallas kernels: none -> 60.1 us  [shards(): pl.pallas_call(functools.partial(kernel, n), out_shape=jax.ShapeDtypeStru...]
    all_to_all x1 -> x0, blocking collectives: 26.6 us -> none  [shards(): lax.all_to_all(eigvecs, 'space', split_axis=3, concat_axis=2, tiled=True)]
    unnamed x8 -> x5, local copies, waits for them, and re-layouts: 22.2 us -> 2.58 us
    dot_general x1 -> x0, matrix products: 11.4 us -> none  [contract_block(): jnp.einsum('tkc,tjc->tkj', spinors.reshape(slices, sources * 32, spinors....]
    slice x1 -> x0, local copies, waits for them, and re-layouts: 11.1 us -> none  [contract_block(): real_part = products[:, :, 0, :, 0, :] + products[:, :, 1, :, 1, :]]
    reshape x1 -> x0, local copies, waits for them, and re-layouts: 10.8 us -> none  [contract_block(): products = products.reshape(slices, sources, 2, 16, 2, count)]
    all_to_all x1 -> x0, local copies, waits for them, and re-layouts: 6.11 us -> none  [shards(): lax.all_to_all(eigvecs, 'space', split_axis=3, concat_axis=2, tiled=True)]
  transfers between devices with their start and end apart: 1 -> 0, of which waited for: 1 -> 0; matrix products, arithmetic and copies ran while one was open for 0% -> 0% of each run, Pallas kernels for 0% -> 0%
where the time goes in v1:
time: 62.9 us; the launch traced here: 62.7 us
  Pallas kernels  60.1 us (96%)
  local copies, waits for them, and re-layouts  2.58 us (4%)
    pallas_call x1, Pallas kernels, shards(): pl.pallas_call(functools.partial(kernel, n), out_shape=jax.ShapeDtypeStru...  60.1 us
    unnamed x5, local copies, waits for them, and re-layouts  2.58 us

profile of v1, /device:TPU:0, one launch (start us, length us, event | category | flops | bytes accessed | tf_op | source)
XLA Modules:
  0.0 62.7 jit_solution(16505057835108140186)
XLA Ops:
  0.0 0.0 copy-start
  0.0 1.1 %copy-done = bf16[2,2,32,3072]{3,2,1,0:T(8,128)(2,1)S(1)} copy-done((bf16[2,2,32,3072]{3,2,1,0:T(8,128)(2,1)S(1)}, bf16[2,2,32,3072]{3,2,1,0:T(8,128)(2,1)}, u32[]{:S(2)}) %copy-start) | copy-done | bytes 786456
  1.1 0.0 copy-start.1
  1.1 0.7 %copy-done.1 = s32[128]{0:T(128)S(1)} copy-done((s32[128]{0:T(128)S(1)}, s32[128]{0:T(128)}, u32[]{:S(2)}) %copy-start.1) | copy-done | bytes 536
  1.8 60.1 %shard_map.37 = bf16[2,32,32,128]{3,2,1,0:T(8,128)(2,1)S(1)} custom-call(s32[128]{0:T(128)S(1)} %copy-done.1, bf16[2,128,32,768]{3,2,1,0:T(8,128)(2,1)} %sol_ref.1, bf16[2,2,32,3072]{3,2,1,0:T(8,128)(2,1)S(1)} %copy-done), custom_call_target="tpu_custom_call" | custom-call | tf_op jit(solution)/shard_map/pallas_call | solution.py:160
  61.9 0.8 %copy.5 = bf16[2,32,32,128]{3,2,1,0:T(8,128)(2,1)} copy(bf16[2,32,32,128]{3,2,1,0:T(8,128)(2,1)S(1)} %shard_map.37) | data formatting | bytes 1048576
Async XLA Ops:
  0.0 1.1 %copy-start = (bf16[2,2,32,3072]{3,2,1,0:T(8,128)(2,1)S(1)}, bf16[2,2,32,3072]{3,2,1,0:T(8,128)(2,1)}, u32[]{:S(2)}) copy-start(bf16[2,2,32,3072]{3,2,1,0:T(8,128)(2,1)} %eig_ref.1) | copy-start | bytes 2359300
  1.1 0.7 %copy-start.1 = (s32[128]{0:T(128)S(1)}, s32[128]{0:T(128)}, u32[]{:S(2)}) copy-start(s32[128]{0:T(128)} %time_ref.1) | copy-start | bytes 1540

commit v2 on v1

v2 whole, which is shorter than its diff:
```python
import functools

import jax
import jax.numpy as jnp
from jax import lax
from jax.experimental import pallas as pl
from jax.experimental.pallas import tpu as pltpu
from jax.sharding import PartitionSpec as P

MESH = pl.DeviceIdType.MESH
LEVELS = 32767.0
PIECES = 2


def kernel(n, pieces, time_hbm, sol_ref, eig_hbm, out_ref, time_ref, eig_ref, sol_v, eig_v, w_v, part, own, code, scale,
           code_in, scale_in, time_sem, load_sem, sol_sem, own_sem, eig_send, eig_recv, code_send, scale_send, code_recv, scale_recv):
    me = lax.axis_index("space")
    slices, sources, spins, cols = sol_v.shape
    count = eig_ref.shape[2]
    vectors = n * count
    owned = sources // n
    piece = owned // pieces
    half = spins // 2
    outer = jnp.where(me < n // 2, me - 1, me + 1)
    is_end = (me == 0) | (me == n - 1)

    barrier = pltpu.get_barrier_semaphore()
    for o in range(1, n):
        pl.semaphore_signal(barrier, inc=1, device_id={"space": lax.rem(me + o, n)}, device_id_type=MESH)

    def block_of(d):
        return pl.ds(pl.multiple_of(d * cols, cols), cols)

    def eig_own(t):
        return pltpu.make_async_copy(eig_hbm.at[t, :, :, block_of(me)], eig_v.at[t, me], own_sem.at[t])

    def eig_load(t):
        return pltpu.make_async_copy(eig_hbm.at[t], eig_ref.at[t], load_sem.at[t])

    def sol_copy(t, d):
        rows = pl.ds(d * owned, owned)
        return pltpu.make_async_copy(sol_ref.at[t, rows], sol_v.at[t, rows], sol_sem.at[t, d])

    def eig_copy(t, o, dst):
        to = lax.rem(me + o, n)
        return pltpu.make_async_remote_copy(
            eig_ref.at[t, :, :, block_of(to)], eig_v.at[t, dst], eig_send.at[t, o], eig_recv.at[t, o],
            device_id={"space": to}, device_id_type=MESH)

    for t in range(slices):
        eig_load(t).start()
    time_copy = pltpu.make_async_copy(time_hbm, time_ref, time_sem)
    time_copy.start()
    for t in range(slices):
        eig_own(t).start()

    def start_sol(t):
        def body(d, _):
            sol_copy(t, d).start()
            return 0
        lax.fori_loop(0, n, body, 0)

    far_first = sorted(range(1, n), key=lambda o: -min(o, n - o))
    eig_load(0).wait()
    pl.semaphore_wait(barrier, n - 1)
    for o in far_first:
        eig_copy(0, o, me).start()
    for t in range(slices):
        start_sol(t)
    for t in range(1, slices):
        eig_load(t).wait()
    time_copy.wait()

    def partial_sum(t, q, dst):
        block = sol_v[t, pl.ds(q * piece, piece)].reshape(piece * spins, cols)
        p = lax.dot_general(block, w_v[t], (((1,), (1,)), ((), ())), preferred_element_type=jnp.float32)
        p = p.reshape(piece, 2, half, 2 * vectors)
        dst[:, :half, :] = p[:, 0, :, :vectors] + p[:, 1, :, vectors:]
        dst[:, half:, :] = p[:, 1, :, :vectors] - p[:, 0, :, vectors:]

    def chunk_copies(way, t, d):
        to = lax.rem(jnp.where(way == 0, me + 1, me + n - 1), n)
        return [
            pltpu.make_async_remote_copy(src.at[t, d], dst.at[way, t, d], s.at[t, d], r.at[way, t, d],
                                         device_id={"space": to}, device_id_type=MESH)
            for src, dst, s, r in ((code, code_in, code_send, code_recv), (scale, scale_in, scale_send, scale_recv))
        ]

    def received(way, t, d):
        for c in chunk_copies(way, t, d):
            c.wait_recv()
        return code_in[way, t, d].astype(jnp.int32).astype(jnp.float32) * scale_in[way, t, d][:1][None]

    def emit(t):
        def body(j, _):
            k = j // (2 * pieces)
            way = jnp.where(me < n // 2, j % 2, 1 - j % 2)
            d = jnp.where(way == 0, n - 1 - k, k)
            q = d * pieces + (j // 2) % pieces

            @pl.when(jnp.where(way == 0, d - me, me - d) > 0)
            def _():
                partial_sum(t, q, part)

                @pl.when(jnp.where(way == 0, me, n - 1 - me) > 0)
                def _():
                    part[...] += received(way, t, q)

                x = part[...]
                top = jnp.maximum(jnp.max(jnp.max(jnp.abs(x), axis=0), axis=0, keepdims=True), 1e-33)
                code[t, q] = jnp.round(x * (LEVELS / top)[None]).astype(jnp.int32).astype(jnp.int16)
                scale[t, q] = jnp.broadcast_to(top * (1.0 / LEVELS), (8, vectors))
                for c in chunk_copies(way, t, q):
                    c.start()
            return 0

        lax.fori_loop(0, 2 * pieces * (n - 1), body, 0)

    def forward(t):
        for o in range(1, n):
            eig_copy(t - 1, o, me).wait_send()
        for o in far_first[::-1]:
            eig_copy(t, o, me).start()

    for t in range(slices):
        if t + 1 < slices:
            @pl.when(is_end)
            def _():
                forward(t + 1)
        else:
            for o in range(1, n):
                eig_copy(t, o, me).wait_send()
        for o in range(1, n):
            source = lax.rem(me + n - o, n)
            if t == 0:
                eig_copy(t, o, source).wait_recv()
            else:
                @pl.when(is_end | (source != outer))
                def _():
                    eig_copy(t, o, source).wait_recv()
        if t + 1 < slices:
            @pl.when(jnp.logical_not(is_end))
            def _():
                o = lax.rem(me + n - outer, n)
                eig_copy(t + 1, o, outer).wait_recv()
                forward(t + 1)
        eig_own(t).wait()
        for c in range(2):
            w_v[t, c * vectors:(c + 1) * vectors, :] = (
                eig_v[t, :, c].astype(jnp.float32).reshape(vectors, cols).astype(jnp.bfloat16))

        def wait_sol(d, _):
            sol_copy(t, d).wait()
            return 0

        lax.fori_loop(0, n, wait_sol, 0)
        emit(t)

        def own_sum(i, _):
            partial_sum(t, me * pieces + i, own.at[t, i])
            return 0

        lax.fori_loop(0, pieces, own_sum, 0)

    def finish(j, _):
        t, i = j // pieces, j % pieces

        @pl.when(me > 0)
        def _():
            own[t, i] += received(0, t, me * pieces + i)

        @pl.when(me < n - 1)
        def _():
            own[t, i] += received(1, t, me * pieces + i)

        now = lax.axis_index("tm") * slices + t
        for b in range(piece):
            sign = jnp.where(now < time_ref[me * owned + i * piece + b], -1.0, 1.0)
            out_ref[t, i * piece + b] = (own[t, i, b] * sign).astype(jnp.bfloat16)
        return 0

    lax.fori_loop(0, slices * pieces, finish, 0)

    def drain(j, _):
        t, q = j // (n * pieces), j % (n * pieces)
        d = q // pieces

        @pl.when(d != me)
        def _():
            for c in chunk_copies(jnp.where(d > me, 0, 1), t, q):
                c.wait_send()
        return 0

    lax.fori_loop(0, slices * n * pieces, drain, 0)


def shards(n, solutions, eigvecs, source_time):
    slices, sources, spins, cols = solutions.shape
    count = eigvecs.shape[2]
    vectors = n * count
    owned = sources // n
    pieces = PIECES if owned % PIECES == 0 else 1
    piece = owned // pieces
    blocks = n * pieces
    dma = pltpu.SemaphoreType.DMA
    return pl.pallas_call(
        functools.partial(kernel, n, pieces),
        out_shape=jax.ShapeDtypeStruct((slices, owned, spins, vectors), jnp.bfloat16),
        in_specs=[
            pl.BlockSpec(memory_space=pltpu.HBM),
            pl.BlockSpec(memory_space=pltpu.HBM),
            pl.BlockSpec(memory_space=pltpu.HBM),
        ],
        out_specs=pl.BlockSpec(memory_space=pltpu.VMEM),
        scratch_shapes=[
            pltpu.SMEM(source_time.shape, jnp.int32),
            pltpu.VMEM(eigvecs.shape, jnp.bfloat16),
            pltpu.VMEM((slices, sources, spins, cols), jnp.bfloat16),
            pltpu.VMEM((slices, n, 2, count, cols), jnp.bfloat16),
            pltpu.VMEM((slices, 2 * vectors, cols), jnp.bfloat16),
            pltpu.VMEM((piece, spins, vectors), jnp.float32),
            pltpu.VMEM((slices, pieces, piece, spins, vectors), jnp.float32),
            pltpu.VMEM((slices, blocks, piece, spins, vectors), jnp.int16),
            pltpu.VMEM((slices, blocks, 8, vectors), jnp.float32),
            pltpu.VMEM((2, slices, blocks, piece, spins, vectors), jnp.int16),
            pltpu.VMEM((2, slices, blocks, 8, vectors), jnp.float32),
            dma,
            dma((slices,)),
            dma((slices, n)),
            dma((slices,)),
            dma((slices, n)),
            dma((slices, n)),
            dma((slices, blocks)),
            dma((slices, blocks)),
            dma((2, slices, blocks)),
            dma((2, slices, blocks)),
        ],
        compiler_params=pltpu.CompilerParams(
            collective_id=0, has_side_effects=True, vmem_limit_bytes=48 << 20),
    )(source_time, solutions, eigvecs)


def solution(mesh):
    return jax.shard_map(
        functools.partial(shards, mesh.shape["space"]),
        mesh=mesh,
        in_specs=(
            P(("cfg", "tm"), None, None, "space"),
            P(("cfg", "tm"), None, "space", None),
            P("cfg"),
        ),
        out_specs=P(("cfg", "tm"), "space", None, None),
        check_vma=False,
    )
```

time: 62.9 us -> 60.6 us (0.963)
  Pallas kernels: 60.1 us -> 57.8 us
    pallas_call x1, Pallas kernels: 60.1 us -> 57.8 us  [shards(): pl.pallas_call(functools.partial(kernel, n, pieces), out_shape=jax.ShapeD...]
where the time goes in v2:
time: 60.6 us; the launch traced here: 60.4 us
  Pallas kernels  57.8 us (95%)
  local copies, waits for them, and re-layouts  2.58 us (4%)
    pallas_call x1, Pallas kernels, shards(): pl.pallas_call(functools.partial(kernel, n, pieces), out_shape=jax.ShapeD...  57.8 us
    unnamed x5, local copies, waits for them, and re-layouts  2.58 us

profile of v2, /device:TPU:0, one launch (start us, length us, event | category | flops | bytes accessed | tf_op | source)
XLA Modules:
  0.0 60.4 jit_solution(2680518415761076725)
XLA Ops:
  0.0 0.0 copy-start
  0.0 1.1 %copy-done = bf16[2,2,32,3072]{3,2,1,0:T(8,128)(2,1)S(1)} copy-done((bf16[2,2,32,3072]{3,2,1,0:T(8,128)(2,1)S(1)}, bf16[2,2,32,3072]{3,2,1,0:T(8,128)(2,1)}, u32[]{:S(2)}) %copy-start) | copy-done | bytes 786456
  1.1 0.0 copy-start.1
  1.1 0.7 %copy-done.1 = s32[128]{0:T(128)S(1)} copy-done((s32[128]{0:T(128)S(1)}, s32[128]{0:T(128)}, u32[]{:S(2)}) %copy-start.1) | copy-done | bytes 536
  1.8 57.8 %shard_map.37 = bf16[2,32,32,128]{3,2,1,0:T(8,128)(2,1)S(1)} custom-call(s32[128]{0:T(128)S(1)} %copy-done.1, bf16[2,128,32,768]{3,2,1,0:T(8,128)(2,1)} %sol_ref.1, bf16[2,2,32,3072]{3,2,1,0:T(8,128)(2,1)S(1)} %copy-done), custom_call_target="tpu_custom_call" | custom-call | tf_op jit(solution)/shard_map/pallas_call | solution.py:206
  59.6 0.8 %copy.5 = bf16[2,32,32,128]{3,2,1,0:T(8,128)(2,1)} copy(bf16[2,32,32,128]{3,2,1,0:T(8,128)(2,1)S(1)} %shard_map.37) | data formatting | bytes 1048576
Async XLA Ops:
  0.0 1.1 %copy-start = (bf16[2,2,32,3072]{3,2,1,0:T(8,128)(2,1)S(1)}, bf16[2,2,32,3072]{3,2,1,0:T(8,128)(2,1)}, u32[]{:S(2)}) copy-start(bf16[2,2,32,3072]{3,2,1,0:T(8,128)(2,1)} %eig_hbm.1) | copy-start | bytes 2359300
  1.1 0.7 %copy-start.1 = (s32[128]{0:T(128)S(1)}, s32[128]{0:T(128)}, u32[]{:S(2)}) copy-start(s32[128]{0:T(128)} %time_hbm.1) | copy-start | bytes 1540

commit v3 on v2

--- a/solution.py
+++ b/solution.py
@@ -9,17 +9,19 @@
 
 MESH = pl.DeviceIdType.MESH
 LEVELS = 32767.0
-PIECES = 2
-
-
-def kernel(n, pieces, time_hbm, sol_ref, eig_hbm, out_ref, time_ref, eig_ref, sol_v, eig_v, w_v, part, own, code, scale,
-           code_in, scale_in, time_sem, load_sem, sol_sem, own_sem, eig_send, eig_recv, code_send, scale_send, code_recv, scale_recv):
+PIECES = 1
+STEP = 0.6931471805599453 / 16
+
+
+def kernel(n, pieces, time_hbm, sol_ref, eig_hbm, out_ref, time_ref, eig_ref, sol_v, eig_v, w_v, part, own, code,
+           code_in, time_sem, load_sem, sol_sem, own_sem, eig_send, eig_recv, code_send, code_recv):
     me = lax.axis_index("space")
     slices, sources, spins, cols = sol_v.shape
     count = eig_ref.shape[2]
     vectors = n * count
     owned = sources // n
     piece = owned // pieces
+    rows = piece * spins
     half = spins // 2
     outer = jnp.where(me < n // 2, me - 1, me + 1)
     is_end = (me == 0) | (me == n - 1)
@@ -78,43 +80,56 @@
         dst[:, :half, :] = p[:, 0, :, :vectors] + p[:, 1, :, vectors:]
         dst[:, half:, :] = p[:, 1, :, :vectors] - p[:, 0, :, vectors:]
 
-    def chunk_copies(way, t, d):
+    def chunk_copy(way, t, q):
         to = lax.rem(jnp.where(way == 0, me + 1, me + n - 1), n)
-        return [
-            pltpu.make_async_remote_copy(src.at[t, d], dst.at[way, t, d], s.at[t, d], r.at[way, t, d],
-                                         device_id={"space": to}, device_id_type=MESH)
-            for src, dst, s, r in ((code, code_in, code_send, code_recv), (scale, scale_in, scale_send, scale_recv))
-        ]
-
-    def received(way, t, d):
-        for c in chunk_copies(way, t, d):
-            c.wait_recv()
-        return code_in[way, t, d].astype(jnp.int32).astype(jnp.float32) * scale_in[way, t, d][:1][None]
-
-    def emit(t):
+        return pltpu.make_async_remote_copy(
+            code.at[t, q], code_in.at[way, t, q], code_send.at[t, q], code_recv.at[way, t, q],
+            device_id={"space": to}, device_id_type=MESH)
+
+    def received(way, t, q):
+        chunk_copy(way, t, q).wait_recv()
+        steps = code_in[way, t, q, rows:].astype(jnp.int32).astype(jnp.float32)[:1]
+        value = code_in[way, t, q, :rows].astype(jnp.int32).astype(jnp.float32) * (jnp.exp(steps * STEP) * (1.0 / LEVELS))
+        return value.reshape(piece, spins, vectors)
+
+    def emit(t, way, d, i):
+        q = d * pieces + i
+        partial_sum(t, q, part)
+
+        @pl.when(jnp.where(way == 0, me, n - 1 - me) > 0)
+        def _():
+            part[...] += received(way, t, q)
+
+        x = part[...].reshape(rows, vectors)
+        top = jnp.maximum(jnp.max(jnp.abs(x), axis=0, keepdims=True), 1e-30)
+        steps = jnp.floor(jnp.log(top) * (1.0 / STEP)) + 2.0
+        code[t, q, :rows] = jnp.round(x * (LEVELS * jnp.exp(steps * -STEP))).astype(jnp.int32).astype(jnp.int16)
+        code[t, q, rows:] = jnp.broadcast_to(steps, (16, vectors)).astype(jnp.int32).astype(jnp.int16)
+        chunk_copy(way, t, q).start()
+
+    def emit_first(t):
         def body(j, _):
             k = j // (2 * pieces)
             way = jnp.where(me < n // 2, j % 2, 1 - j % 2)
             d = jnp.where(way == 0, n - 1 - k, k)
-            q = d * pieces + (j // 2) % pieces
-
-            @pl.when(jnp.where(way == 0, d - me, me - d) > 0)
+            least = jnp.where(is_end, 1, 0)
+
+            @pl.when(jnp.where(way == 0, d - me, me - d) > least)
             def _():
-                partial_sum(t, q, part)
-
-                @pl.when(jnp.where(way == 0, me, n - 1 - me) > 0)
-                def _():
-                    part[...] += received(way, t, q)
-
-                x = part[...]
-                top = jnp.maximum(jnp.max(jnp.max(jnp.abs(x), axis=0), axis=0, keepdims=True), 1e-33)
-                code[t, q] = jnp.round(x * (LEVELS / top)[None]).astype(jnp.int32).astype(jnp.int16)
-                scale[t, q] = jnp.broadcast_to(top * (1.0 / LEVELS), (8, vectors))
-                for c in chunk_copies(way, t, q):
-                    c.start()
+                emit(t, way, d, (j // 2) % pieces)
             return 0
 
         lax.fori_loop(0, 2 * pieces * (n - 1), body, 0)
+
+    def emit_last():
+        def body(j, _):
+            way = jnp.where(me == 0, 0, 1)
+            emit(j // pieces, way, jnp.where(me == 0, 1, n - 2), j % pieces)
+            return 0
+
+        @pl.when(is_end)
+        def _():
+            lax.fori_loop(0, slices * pieces, body, 0)
 
     def forward(t):
         for o in range(1, n):
@@ -154,7 +169,9 @@
             return 0
 
         lax.fori_loop(0, n, wait_sol, 0)
-        emit(t)
+        emit_first(t)
+        if t + 1 == slices:
+            emit_last()
 
         def own_sum(i, _):
             partial_sum(t, me * pieces + i, own.at[t, i])
@@ -187,8 +204,7 @@
 
         @pl.when(d != me)
         def _():
-            for c in chunk_copies(jnp.where(d > me, 0, 1), t, q):
-                c.wait_send()
+            chunk_copy(jnp.where(d > me, 0, 1), t, q).wait_send()
         return 0
 
     lax.fori_loop(0, slices * n * pieces, drain, 0)
@@ -220,10 +236,8 @@
             pltpu.VMEM((slices, 2 * vectors, cols), jnp.bfloat16),
             pltpu.VMEM((piece, spins, vectors), jnp.float32),
             pltpu.VMEM((slices, pieces, piece, spins, vectors), jnp.float32),
-            pltpu.VMEM((slices, blocks, piece, spins, vectors), jnp.int16),
-            pltpu.VMEM((slices, blocks, 8, vectors), jnp.float32),
-            pltpu.VMEM((2, slices, blocks, piece, spins, vectors), jnp.int16),
-            pltpu.VMEM((2, slices, blocks, 8, vectors), jnp.float32),
+            pltpu.VMEM((slices, blocks, piece * spins + 16, vectors), jnp.int16),
+            pltpu.VMEM((2, slices, blocks, piece * spins + 16, vectors), jnp.int16),
             dma,
             dma((slices,)),
             dma((slices, n)),
@@ -231,8 +245,6 @@
             dma((slices, n)),
             dma((slices, n)),
             dma((slices, blocks)),
-            dma((slices, blocks)),
-            dma((2, slices, blocks)),
             dma((2, slices, blocks)),
         ],
         compiler_params=pltpu.CompilerParams(

time: 60.6 us -> 55.2 us (0.911)
  Pallas kernels: 57.8 us -> 52.5 us
    pallas_call x1, Pallas kernels: 57.8 us -> 52.5 us  [shards(): pl.pallas_call(functools.partial(kernel, n, pieces), out_shape=jax.ShapeD...]
where the time goes in v3:
time: 55.2 us; the launch traced here: 55.1 us
  Pallas kernels  52.5 us (95%)
  local copies, waits for them, and re-layouts  2.58 us (5%)
    pallas_call x1, Pallas kernels, shards(): pl.pallas_call(functools.partial(kernel, n, pieces), out_shape=jax.ShapeD...  52.5 us
    unnamed x5, local copies, waits for them, and re-layouts  2.58 us

profile of v3, /device:TPU:0, one launch (start us, length us, event | category | flops | bytes accessed | tf_op | source)
XLA Modules:
  0.0 55.1 jit_solution(8181049098283432933)
XLA Ops:
  0.0 0.0 copy-start
  0.0 1.1 %copy-done = bf16[2,2,32,3072]{3,2,1,0:T(8,128)(2,1)S(1)} copy-done((bf16[2,2,32,3072]{3,2,1,0:T(8,128)(2,1)S(1)}, bf16[2,2,32,3072]{3,2,1,0:T(8,128)(2,1)}, u32[]{:S(2)}) %copy-start) | copy-done | bytes 786456
  1.1 0.0 copy-start.1
  1.1 0.7 %copy-done.1 = s32[128]{0:T(128)S(1)} copy-done((s32[128]{0:T(128)S(1)}, s32[128]{0:T(128)}, u32[]{:S(2)}) %copy-start.1) | copy-done | bytes 536
  1.8 52.5 %shard_map.37 = bf16[2,32,32,128]{3,2,1,0:T(8,128)(2,1)S(1)} custom-call(s32[128]{0:T(128)S(1)} %copy-done.1, bf16[2,128,32,768]{3,2,1,0:T(8,128)(2,1)} %sol_ref.1, bf16[2,2,32,3072]{3,2,1,0:T(8,128)(2,1)S(1)} %copy-done), custom_call_target="tpu_custom_call" | custom-call | tf_op jit(solution)/shard_map/pallas_call | solution.py:222
  54.3 0.8 %copy.5 = bf16[2,32,32,128]{3,2,1,0:T(8,128)(2,1)} copy(bf16[2,32,32,128]{3,2,1,0:T(8,128)(2,1)S(1)} %shard_map.37) | data formatting | bytes 1048576
Async XLA Ops:
  0.0 1.1 %copy-start = (bf16[2,2,32,3072]{3,2,1,0:T(8,128)(2,1)S(1)}, bf16[2,2,32,3072]{3,2,1,0:T(8,128)(2,1)}, u32[]{:S(2)}) copy-start(bf16[2,2,32,3072]{3,2,1,0:T(8,128)(2,1)} %eig_hbm.1) | copy-start | bytes 2359300
  1.1 0.7 %copy-start.1 = (s32[128]{0:T(128)S(1)}, s32[128]{0:T(128)}, u32[]{:S(2)}) copy-start(s32[128]{0:T(128)} %time_hbm.1) | copy-start | bytes 1540

commit v4 on v3

--- a/solution.py
+++ b/solution.py
@@ -14,7 +14,7 @@
 
 
 def kernel(n, pieces, time_hbm, sol_ref, eig_hbm, out_ref, time_ref, eig_ref, sol_v, eig_v, w_v, part, own, code,
-           code_in, time_sem, load_sem, sol_sem, own_sem, eig_send, eig_recv, code_send, code_recv):
+           code_in, time_sem, load_sem, sol_sem, own_sem, eig_send, eig_recv, code_send, code_recv, wave):
     me = lax.axis_index("space")
     slices, sources, spins, cols = sol_v.shape
     count = eig_ref.shape[2]
@@ -27,8 +27,17 @@
     is_end = (me == 0) | (me == n - 1)
 
     barrier = pltpu.get_barrier_semaphore()
-    for o in range(1, n):
-        pl.semaphore_signal(barrier, inc=1, device_id={"space": lax.rem(me + o, n)}, device_id_type=MESH)
+
+    def tell(semaphore, where):
+        pl.semaphore_signal(semaphore, inc=1, device_id={"space": lax.rem(where + n, n)}, device_id_type=MESH)
+
+    @pl.when(me > 0)
+    def _():
+        tell(barrier, me - 1)
+
+    @pl.when(me < n - 1)
+    def _():
+        tell(barrier, me + 1)
 
     def block_of(d):
         return pl.ds(pl.multiple_of(d * cols, cols), cols)
@@ -64,9 +73,44 @@
 
     far_first = sorted(range(1, n), key=lambda o: -min(o, n - o))
     eig_load(0).wait()
-    pl.semaphore_wait(barrier, n - 1)
+    pl.semaphore_wait(barrier, jnp.where(is_end, 1, 2))
+
+    def is_near(o):
+        return jnp.abs(lax.rem(me + o, n) - me) == 1
+
+    @pl.when(me == 0)
+    def _():
+        tell(wave.at[0], me + 1)
+
+    @pl.when(me == n - 1)
+    def _():
+        tell(wave.at[1], me - 1)
+
     for o in far_first:
-        eig_copy(0, o, me).start()
+        @pl.when(is_near(o))
+        def _():
+            eig_copy(0, o, me).start()
+
+    @pl.when(me > 0)
+    def _():
+        pl.semaphore_wait(wave.at[0], 1)
+
+        @pl.when(me < n - 1)
+        def _():
+            tell(wave.at[0], me + 1)
+
+    @pl.when(me < n - 1)
+    def _():
+        pl.semaphore_wait(wave.at[1], 1)
+
+        @pl.when(me > 0)
+        def _():
+            tell(wave.at[1], me - 1)
+
+    for o in far_first:
+        @pl.when(jnp.logical_not(is_near(o)))
+        def _():
+            eig_copy(0, o, me).start()
     for t in range(slices):
         start_sol(t)
     for t in range(1, slices):
@@ -246,6 +290,7 @@
             dma((slices, n)),
             dma((slices, blocks)),
             dma((2, slices, blocks)),
+            pltpu.SemaphoreType.REGULAR((2,)),
         ],
         compiler_params=pltpu.CompilerParams(
             collective_id=0, has_side_effects=True, vmem_limit_bytes=48 << 20),

time: 55.2 us -> 57.2 us (1.036)
  Pallas kernels: 52.5 us -> 54.5 us
    pallas_call x1, Pallas kernels: 52.5 us -> 54.5 us  [shards(): pl.pallas_call(functools.partial(kernel, n, pieces), out_shape=jax.ShapeD...]
where the time goes in v4:
time: 57.2 us; the launch traced here: 57.1 us
  Pallas kernels  54.5 us (95%)
  local copies, waits for them, and re-layouts  2.58 us (5%)
    pallas_call x1, Pallas kernels, shards(): pl.pallas_call(functools.partial(kernel, n, pieces), out_shape=jax.ShapeD...  54.5 us
    unnamed x5, local copies, waits for them, and re-layouts  2.58 us

profile of v4, /device:TPU:0, one launch (start us, length us, event | category | flops | bytes accessed | tf_op | source)
XLA Modules:
  0.0 57.1 jit_solution(14907580781136414981)
XLA Ops:
  0.0 0.0 copy-start
  0.0 1.1 %copy-done = bf16[2,2,32,3072]{3,2,1,0:T(8,128)(2,1)S(1)} copy-done((bf16[2,2,32,3072]{3,2,1,0:T(8,128)(2,1)S(1)}, bf16[2,2,32,3072]{3,2,1,0:T(8,128)(2,1)}, u32[]{:S(2)}) %copy-start) | copy-done | bytes 786456
  1.1 0.0 copy-start.1
  1.1 0.7 %copy-done.1 = s32[128]{0:T(128)S(1)} copy-done((s32[128]{0:T(128)S(1)}, s32[128]{0:T(128)}, u32[]{:S(2)}) %copy-start.1) | copy-done | bytes 536
  1.8 54.5 %shard_map.37 = bf16[2,32,32,128]{3,2,1,0:T(8,128)(2,1)S(1)} custom-call(s32[128]{0:T(128)S(1)} %copy-done.1, bf16[2,128,32,768]{3,2,1,0:T(8,128)(2,1)} %sol_ref.1, bf16[2,2,32,3072]{3,2,1,0:T(8,128)(2,1)S(1)} %copy-done), custom_call_target="tpu_custom_call" | custom-call | tf_op jit(solution)/shard_map/pallas_call | solution.py:266
  56.3 0.8 %copy.5 = bf16[2,32,32,128]{3,2,1,0:T(8,128)(2,1)} copy(bf16[2,32,32,128]{3,2,1,0:T(8,128)(2,1)S(1)} %shard_map.37) | data formatting | bytes 1048576
Async XLA Ops:
  0.0 1.1 %copy-start = (bf16[2,2,32,3072]{3,2,1,0:T(8,128)(2,1)S(1)}, bf16[2,2,32,3072]{3,2,1,0:T(8,128)(2,1)}, u32[]{:S(2)}) copy-start(bf16[2,2,32,3072]{3,2,1,0:T(8,128)(2,1)} %eig_hbm.1) | copy-start | bytes 2359300
  1.1 0.7 %copy-start.1 = (s32[128]{0:T(128)S(1)}, s32[128]{0:T(128)}, u32[]{:S(2)}) copy-start(s32[128]{0:T(128)} %time_hbm.1) | copy-start | bytes 1540
